TPU v7x, 256 devices: a whole 4x4x8 slice. The times are simulated.
256 devices in a mesh: lon: 64 (over y, x_lo, z), lat: 4 (over x_hi, core).
Axes of the slice: x: 4 (x_hi: 2, x_lo: 2; x = x_hi * 2 + x_lo), y: 4, z: 8, core: 2. Of those that a mesh axis runs over, the one named last changes fastest.
Arguments:
- perturbation: float32 [80, 1024, 4096], P(None, 'lon', 'lat'), may hold values from -6 to 6
- weight_table: float32 [8, 2048], P(None, 'lat'), may hold values from 0.1 to 1
- band_index: int32 [13], replicated, may hold values from 0 to 7
Outputs:
- localized: float32 [80, 1024, 4096], P(None, 'lon', 'lat')
Inputs may be any that keep to these rules, and one draw needn't show every extreme that they name: `band_index`: each entry names a row of weight_table.
All inputs are finite; a program needn't handle non-finite values.
Results may differ from a plain program's by a relative error of at most 0.00005.
Values sent between devices are 32-bit elements; how exact they have to be, the bound alone decides.
A program may use at most 128 MiB of HBM per device.

v0:
```python
import math

import jax
import jax.numpy as jnp
from jax import lax
from jax.sharding import PartitionSpec as P

LEVELS = 4
TABLE = 8


root_three = math.sqrt(3.0)
low_taps = [
    (1.0 + root_three) / (4.0 * math.sqrt(2.0)),
    (3.0 + root_three) / (4.0 * math.sqrt(2.0)),
    (3.0 - root_three) / (4.0 * math.sqrt(2.0)),
    (1.0 - root_three) / (4.0 * math.sqrt(2.0)),
]
high_taps = [low_taps[3], -low_taps[2], low_taps[1], -low_taps[0]]


def from_behind(x, axis, by):
    size = lax.axis_size(axis)
    return lax.ppermute(x, axis, [(i, (i + by) % size) for i in range(size)])


def passed_along(x, axis, by):
    size = lax.axis_size(axis)
    pairs = [(i, i + by) for i in range(size) if 0 <= i + by < size]
    return lax.ppermute(x, axis, pairs)


def tap_matrix(offset, taps):
    result = jnp.zeros(offset.shape, jnp.float32)
    for tap in range(4):
        result = result + taps[tap] * (offset == tap).astype(jnp.float32)
    return result


def lat_apply(field, matrix):
    return jnp.einsum("mcr,rk->mck", field, matrix, precision=lax.Precision.HIGHEST)


def lat_filter(field, low_count, high_count):
    rows = field.shape[2]
    row_ids = jnp.arange(rows, dtype=jnp.int32)[:, None]
    low_cols = jnp.arange(low_count // 2, dtype=jnp.int32)[None, :]
    high_cols = jnp.arange(high_count // 2, dtype=jnp.int32)[None, :]
    matrix = jnp.concatenate(
        [
            tap_matrix(row_ids - 2 * low_cols, low_taps),
            tap_matrix(row_ids - 2 * high_cols, high_taps),
        ],
        1,
    )
    result = lat_apply(field, matrix)
    return (result[:, :, : low_count // 2], result[:, :, low_count // 2 :])


def lat_join_ext(low_ext, high_ext):
    rows = low_ext.shape[2]
    row_ids = jnp.arange(rows, dtype=jnp.int32)[:, None]
    col_ids = jnp.arange(2 * (rows - 1), dtype=jnp.int32)[None, :]
    offset = col_ids - 2 * row_ids + 2
    matrix = jnp.concatenate([tap_matrix(offset, low_taps), tap_matrix(offset, high_taps)], 0)
    return lat_apply(jnp.concatenate([low_ext, high_ext], 2), matrix)


def lon_split(extended):
    shape = extended.shape
    pairs = extended.reshape(shape[0], shape[1] // 2, 2, shape[2])
    even = pairs[:, :, 0]
    odd = pairs[:, :, 1]

    def combine(taps):
        return (
            taps[0] * even[:, :-1]
            + taps[1] * odd[:, :-1]
            + taps[2] * even[:, 1:]
            + taps[3] * odd[:, 1:]
        )

    return (combine(low_taps), combine(high_taps))


def synthesize(low, high, prev_low, prev_high, axis):
    even = (
        low_taps[0] * low + low_taps[2] * prev_low + high_taps[0] * high + high_taps[2] * prev_high
    )
    odd = (
        low_taps[1] * low + low_taps[3] * prev_low + high_taps[1] * high + high_taps[3] * prev_high
    )
    paired = jnp.stack([even, odd], axis + 1)
    shape = list(low.shape)
    shape[axis] = shape[axis] * 2
    return paired.reshape(shape)


def profile(weight_table, band_index, entry, level):
    picked = (jnp.arange(TABLE, dtype=jnp.int32) == band_index[entry]).astype(jnp.float32)
    columns = weight_table[:, :: 2**level]
    return jnp.sum(picked[:, None] * columns, 0)[None, None, :]


def split_cycle_lon(field):
    beyond = from_behind(field[:, :2], "lon", -1)
    return lon_split(jnp.concatenate([field, beyond], 1))


def split_lat(lon_low, lon_high, level, weight_table, band_index):
    beyond = passed_along(jnp.stack([lon_low[:, :, :2], lon_high[:, :, :2]]), "lat", -1)
    count = lon_low.shape[2]
    ext_low = jnp.concatenate([lon_low, beyond[0]], 2)
    ext_high = jnp.concatenate([lon_high, beyond[1]], 2)
    coarse, band_zero = lat_filter(ext_low, count, count)
    band_one, band_two = lat_filter(ext_high, count, count)
    bands = [band_zero, band_one, band_two]
    weighted = [
        bands[b] * profile(weight_table, band_index, 3 * level + b, level) for b in range(3)
    ]
    return (coarse, weighted)


def join_lat(coarse, bands):
    stacked = jnp.stack(
        [coarse[:, :, -1:], bands[0][:, :, -1:], bands[1][:, :, -1:], bands[2][:, :, -1:]]
    )
    before = passed_along(stacked, "lat", 1)
    members = [coarse, bands[0], bands[1], bands[2]]
    extended = [jnp.concatenate([before[i], members[i]], 2) for i in range(4)]
    lon_low = lat_join_ext(extended[0], extended[1])
    lon_high = lat_join_ext(extended[2], extended[3])
    return (lon_low, lon_high)


def join_cycle_lon(lon_low, lon_high):
    before = from_behind(jnp.stack([lon_low[:, -1:], lon_high[:, -1:]]), "lon", 1)
    prev_low = jnp.concatenate([before[0], lon_low[:, :-1]], 1)
    prev_high = jnp.concatenate([before[1], lon_high[:, :-1]], 1)
    return synthesize(lon_low, lon_high, prev_low, prev_high, 1)


def per_device(perturbation, weight_table, band_index):
    current = perturbation
    details = []
    sharded_levels = LEVELS
    for level in range(sharded_levels):
        lon_low, lon_high = split_cycle_lon(current)
        current, weighted = split_lat(lon_low, lon_high, level, weight_table, band_index)
        details.append(weighted)
    current = current * profile(weight_table, band_index, 3 * LEVELS, LEVELS - 1)
    for level in reversed(range(sharded_levels)):
        lon_low, lon_high = join_lat(current, details[level])
        current = join_cycle_lon(lon_low, lon_high)
    return current


def solution(mesh):
    placed = (P(None, "lon", "lat"), P(None, "lat"), P())
    return jax.shard_map(
        per_device, mesh=mesh, in_specs=placed, out_specs=P(None, "lon", "lat"), check_vma=False
    )
```

profile of v0, /device:TPU:1, one launch (start us, length us, event | category | flops | bytes accessed | tf_op | source)
XLA Modules:
  0.0 282.6 jit_solution(17068141785426257769)
XLA Ops:
  0.0 5.5 %copy.392 = f32[80,16,1024]{2,0,1:T(8,128)S(1)} copy(f32[80,16,1024]{2,1,0:T(8,128)} %param.3) | data formatting | bytes 10485760 | tf_op args[0]
  8.0 10.1 %collective-permute-start = (f32[80,2,1024]{2,0,1:T(8,128)S(1)}, f32[80,2,1024]{2,0,1:T(8,128)S(1)}, u32[]{:S(2)}, u32[]{:S(2)}) collective-permute-start(f32[80,2,1024]{2,0,1:T(8,128)S(1)} %slice.533), channel_id=1, source_target_pairs={{0,252},{4,0},{8,4},{12,8},{16,12},{20,16},{24,20},{28,24},{32,28}... | collective-permute-start | bytes 1966088 | tf_op jit(solution)/shard_map/ppermute | solution.py:24
  33.9 3.7 %copy_bitcast_fusion = (f32[80,9,1024]{2,1,0:T(8,128)S(1)}, f32[80,9,1024]{2,1,0:T(8,128)S(1)}) fusion(f32[80,9,1,1024]{3,0,2,1:T(8,128)S(1)} %get-tuple-element.23, f32[80,9,1,1024]{3,0,2,1:T(8,128)S(1)} %get-tuple-element.22), kind=kLoop, calls=%fused_computation.2 | loop fusion | bytes 11796480 | tf_op jit(solution)/shard_map/squeeze | solution.py:73
  50.2 14.4 %fusion.1 = f32[80,8,1024]{2,1,0:T(8,128)} fusion(f32[1026,512]{1,0:T(8,128)} %get-tuple-element.97, f32[1026,512]{1,0:T(8,128)} %get-tuple-element.96, f32[80,8,2]{2,1,0:T(8,128)S(1)} %bitcast.244, f32[80,8,1024]{2,1,0:T(8,128)} %copy-done.4), kind=kOutput, calls=%fused_computation.7 | convolution fusion | flops 8070499328 | bytes 9450496 | tf_op jit(solution)/shard_map/mcr,rk->mck/dot_general | solution.py:41
  66.7 5.8 %collective-permute-start.2 = (f32[80,2,512]{2,1,0:T(2,128)}, f32[80,2,512]{2,1,0:T(2,128)S(1)}, u32[]{:S(2)}, u32[]{:S(2)}) collective-permute-start(f32[80,2,512]{2,1,0:T(2,128)} %slice.544), channel_id=1, source_target_pairs={{0,252},{4,0},{8,4},{12,8},{16,12},{20,16},{24,20},{28,24},{32,28}... | collective-permute-start | bytes 983048 | tf_op jit(solution)/shard_map/ppermute | solution.py:24
  75.4 3.5 %collective-permute-done.2 = f32[80,2,512]{2,1,0:T(2,128)S(1)} collective-permute-done((f32[80,2,512]{2,1,0:T(2,128)}, f32[80,2,512]{2,1,0:T(2,128)S(1)}, u32[]{:S(2)}, u32[]{:S(2)}) %collective-permute-start.2) | collective-permute-done | bytes 327712 | tf_op jit(solution)/shard_map/ppermute | solution.py:24
  82.9 7.9 %collective-permute-done.3 = f32[2,80,4,2]{3,1,2,0:T(8,128)S(1)} collective-permute-done((f32[2,80,4,2]{3,1,2,0:T(8,128)S(1)}, f32[2,80,4,2]{3,1,2,0:T(8,128)S(1)}, u32[]{:S(2)}, u32[]{:S(2)}) %collective-permute-start.3) | collective-permute-done | bytes 5152 | tf_op jit(solution)/shard_map/ppermute | solution.py:30
  92.6 10.4 %collective-permute-start.4 = (f32[80,2,256]{2,0,1:T(8,128)S(1)}, f32[80,2,256]{2,0,1:T(8,128)S(1)}, u32[]{:S(2)}, u32[]{:S(2)}) collective-permute-start(f32[80,2,256]{2,0,1:T(8,128)S(1)} %slice.555), channel_id=1, source_target_pairs={{0,252},{4,0},{8,4},{12,8},{16,12},{20,16},{24,20},{28,24},{32,28}... | collective-permute-start | bytes 491528 | tf_op jit(solution)/shard_map/ppermute | solution.py:24
  107.5 6.1 %collective-permute-done.5 = f32[2,80,2,2]{3,1,2,0:T(8,128)S(1)} collective-permute-done((f32[2,80,2,2]{3,1,2,0:T(8,128)S(1)}, f32[2,80,2,2]{3,1,2,0:T(8,128)S(1)}, u32[]{:S(2)}, u32[]{:S(2)}) %collective-permute-start.5) | collective-permute-done | bytes 2592 | tf_op jit(solution)/shard_map/ppermute | solution.py:30
  114.1 6.2 %collective-permute-start.6 = (f32[80,2,128]{2,0,1:T(8,128)S(1)}, f32[80,2,128]{2,0,1:T(8,128)S(1)}, u32[]{:S(2)}, u32[]{:S(2)}) collective-permute-start(f32[80,2,128]{2,0,1:T(8,128)S(1)} %get-tuple-element.62), channel_id=1, source_target_pairs={{0,252},{4,0},{8,4},{12,8},{16,12},{20,16},{24,20},{28,24},{32,28}... | collective-permute-start | bytes 245768 | tf_op jit(solution)/shard_map/ppermute | solution.py:24
  124.2 4.3 %collective-permute-done.7 = f32[2,80,1,2]{1,3,2,0:T(2,128)S(1)} collective-permute-done((f32[2,80,1,2]{1,3,2,0:T(2,128)S(1)}, f32[2,80,1,2]{1,3,2,0:T(2,128)S(1)}, u32[]{:S(2)}, u32[]{:S(2)}) %collective-permute-start.7) | collective-permute-done | bytes 1312 | tf_op jit(solution)/shard_map/ppermute | solution.py:30
  134.6 8.5 %collective-permute-done.9 = f32[2,80,1,128]{3,1,2,0:T(8,128)S(1)} collective-permute-done((f32[2,80,1,128]{3,1,2,0:T(8,128)S(1)}, f32[2,80,1,128]{3,1,2,0:T(8,128)S(1)}, u32[]{:S(2)}, u32[]{:S(2)}) %collective-permute-start.9) | collective-permute-done | bytes 81952 | tf_op jit(solution)/shard_map/ppermute | solution.py:24
  143.3 6.0 %collective-permute-start.10 = (f32[4,80,2,1]{1,2,3,0:T(2,128)S(1)}, f32[4,80,2,1]{1,2,3,0:T(2,128)S(1)}, u32[]{:S(2)}, u32[]{:S(2)}) collective-permute-start(f32[4,80,2,1]{1,2,3,0:T(2,128)S(1)} %pad_maximum_fusion.28), channel_id=1, source_target_pairs={{0,1},{1,2},{2,3},{4,5},{5,6},{6,7},{8,9},{9,10},{10,11},{12,13},{... | collective-permute-start | bytes 7688 | tf_op jit(solution)/shard_map/ppermute | solution.py:30
  152.2 7.9 %collective-permute-done.11 = f32[2,80,1,256]{3,1,2,0:T(8,128)S(1)} collective-permute-done((f32[2,80,1,256]{3,1,2,0:T(8,128)S(1)}, f32[2,80,1,256]{3,1,2,0:T(8,128)S(1)}, u32[]{:S(2)}, u32[]{:S(2)}) %collective-permute-start.11) | collective-permute-done | bytes 163872 | tf_op jit(solution)/shard_map/ppermute | solution.py:24
  160.5 7.0 %collective-permute-start.12 = (f32[4,80,4,1]{1,2,3,0:T(4,128)S(1)}, f32[4,80,4,1]{1,2,3,0:T(4,128)S(1)}, u32[]{:S(2)}, u32[]{:S(2)}) collective-permute-start(f32[4,80,4,1]{1,2,3,0:T(4,128)S(1)} %pad_maximum_fusion.27), channel_id=1, source_target_pairs={{0,1},{1,2},{2,3},{4,5},{5,6},{6,7},{8,9},{9,10},{10,11},{12,13},{... | collective-permute-start | bytes 15368 | tf_op jit(solution)/shard_map/ppermute | solution.py:30
  177.9 13.1 %fusion = f32[80,8,1024]{2,1,0:T(8,128)S(1)} fusion(f32[1026,512]{1,0:T(8,128)} %get-tuple-element.97, f32[1026,512]{1,0:T(8,128)} %get-tuple-element.96, f32[80,8,2]{2,1,0:T(8,128)} %bitcast.243, f32[80,8,1024]{2,1,0:T(8,128)S(1)} %copy-done.3), kind=kOutput, calls=%fused_computation.6 | convolution fusion | flops 8070499328 | bytes 9450496 | tf_op jit(solution)/shard_map/mcr,rk->mck/dot_general | solution.py:41
  201.9 5.4 %collective-permute-start.14 = (f32[4,80,8,1]{1,2,3,0:T(8,128)S(1)}, f32[4,80,8,1]{1,2,3,0:T(8,128)S(1)}, u32[]{:S(2)}, u32[]{:S(2)}) collective-permute-start(f32[4,80,8,1]{1,2,3,0:T(8,128)S(1)} %pad_maximum_fusion.26), channel_id=1, source_target_pairs={{0,1},{1,2},{2,3},{4,5},{5,6},{6,7},{8,9},{9,10},{10,11},{12,13},{... | collective-permute-start | bytes 30728 | tf_op jit(solution)/shard_map/ppermute | solution.py:30
  207.3 3.6 %select_add_fusion.1 = (f32[513,1024]{1,0:T(8,128)}, f32[513,1024]{1,0:T(8,128)}) fusion(s32[513]{0:T(1024)S(1)} %iota_multiply_fusion), kind=kLoop, calls=%fused_computation.24 | loop fusion | flops 10506240 | bytes 4204548 | tf_op jit(solution)/shard_map/add | solution.py:36
  213.1 4.5 %concatenate.139 = f32[80,8,1026]{2,1,0:T(8,128)} concatenate(f32[80,8,1]{2,1,0:T(8,128)S(1)} %copy.423, f32[80,8,512]{2,1,0:T(8,128)} %copy.424, f32[80,8,1]{2,1,0:T(8,128)S(1)} %copy.425, f32[80,8,512]{2,1,0:T(8,128)S(1)} %get-tuple-element.27), dimensions={2} | concatenate | bytes 5253120 | tf_op jit(solution)/shard_map/concatenate | solution.py:66
  217.6 13.6 %fusion.3 = f32[80,8,1024]{2,1,0:T(8,128)S(1)} fusion(f32[80,8,1026]{2,1,0:T(8,128)} %concatenate.139, f32[513,1024]{1,0:T(8,128)} %get-tuple-element.83, f32[513,1024]{1,0:T(8,128)} %get-tuple-element.82), kind=kOutput, calls=%fused_computation.9 | convolution fusion | flops 8069842944 | bytes 9450496 | tf_op jit(solution)/shard_map/mcr,rk->mck/dot_general | solution.py:41
  232.7 4.5 %concatenate.141 = f32[80,8,1026]{2,1,0:T(8,128)} concatenate(f32[80,8,1]{2,1,0:T(8,128)S(1)} %copy.426, f32[80,8,512]{2,1,0:T(8,128)} %get-tuple-element.28, f32[80,8,1]{2,1,0:T(8,128)S(1)} %copy.427, f32[80,8,512]{2,1,0:T(8,128)} %copy-done.2), dimensions={2} | concatenate | bytes 5253120 | tf_op jit(solution)/shard_map/concatenate | solution.py:66
  237.1 13.7 %fusion.2 = f32[80,8,1024]{2,1,0:T(8,128)S(1)} fusion(f32[80,8,1026]{2,1,0:T(8,128)} %concatenate.141, f32[513,1024]{1,0:T(8,128)} %get-tuple-element.83, f32[513,1024]{1,0:T(8,128)} %get-tuple-element.82), kind=kOutput, calls=%fused_computation.8 | convolution fusion | flops 8069842944 | bytes 9450496 | tf_op jit(solution)/shard_map/mcr,rk->mck/dot_general | solution.py:41
  252.1 18.2 %collective-permute-done.15 = f32[2,80,1,1024]{3,2,1,0:T(1,128)S(1)} collective-permute-done((f32[2,80,1,1024]{3,2,1,0:T(1,128)S(1)}, f32[2,80,1,1024]{3,2,1,0:T(1,128)S(1)}, u32[]{:S(2)}, u32[]{:S(2)}) %collective-permute-start.15) | collective-permute-done | bytes 655392 | tf_op jit(solution)/shard_map/ppermute | solution.py:24
  276.8 5.4 %copy.429 = f32[80,16,1024]{2,1,0:T(8,128)} copy(f32[80,16,1024]{2,0,1:T(8,128)S(1)} %bitcast.229) | data formatting | bytes 10485760 | tf_op jit(solution)/shard_map/reshape | solution.py:96
  (204 shorter events, 92.0 us)
Async XLA Ops:
  0.0 18.0 %copy-start.12 = (f32[8,512]{1,0:T(8,128)S(1)}, f32[8,512]{1,0:T(8,128)}, u32[]{:S(2)}) copy-start(f32[8,512]{1,0:T(8,128)} %param.4) | copy-start | bytes 49156
  0.0 18.6 %copy-start.11 = (s32[13]{0:T(128)S(1)}, s32[13]{0:T(128)}, u32[]{:S(2)}) copy-start(s32[13]{0:T(128)} %param.5) | copy-start | bytes 160
  8.0 23.9 %collective-permute-start = (f32[80,2,1024]{2,0,1:T(8,128)S(1)}, f32[80,2,1024]{2,0,1:T(8,128)S(1)}, u32[]{:S(2)}, u32[]{:S(2)}) collective-permute-start(f32[80,2,1024]{2,0,1:T(8,128)S(1)} %slice.533), channel_id=1, source_target_pairs={{0,252},{4,0},{8,4},{12,8},{16,12},{20,16},{24,20},{28,24},{32,28}... | collective-permute-start | bytes 1966088 | tf_op jit(solution)/shard_map/ppermute | solution.py:24
  43.3 6.7 %collective-permute-start.1 = (f32[2,80,8,2]{1,2,3,0:T(8,128)S(1)}, f32[2,80,8,2]{1,2,3,0:T(8,128)S(1)}, u32[]{:S(2)}, u32[]{:S(2)}) collective-permute-start(f32[2,80,8,2]{1,2,3,0:T(8,128)S(1)} %pad_maximum_fusion.25), channel_id=1, source_target_pairs={{1,0},{2,1},{3,2},{5,4},{6,5},{7,6},{9,8},{10,9},{11,10},{13,12},{... | collective-permute-start | bytes 30728 | tf_op jit(solution)/shard_map/ppermute | solution.py:30
  66.7 12.1 %collective-permute-start.2 = (f32[80,2,512]{2,1,0:T(2,128)}, f32[80,2,512]{2,1,0:T(2,128)S(1)}, u32[]{:S(2)}, u32[]{:S(2)}) collective-permute-start(f32[80,2,512]{2,1,0:T(2,128)} %slice.544), channel_id=1, source_target_pairs={{0,252},{4,0},{8,4},{12,8},{16,12},{20,16},{24,20},{28,24},{32,28}... | collective-permute-start | bytes 983048 | tf_op jit(solution)/shard_map/ppermute | solution.py:24
  80.9 9.9 %collective-permute-start.3 = (f32[2,80,4,2]{3,1,2,0:T(8,128)S(1)}, f32[2,80,4,2]{3,1,2,0:T(8,128)S(1)}, u32[]{:S(2)}, u32[]{:S(2)}) collective-permute-start(f32[2,80,4,2]{3,1,2,0:T(8,128)S(1)} %pad_maximum_fusion.10), channel_id=1, source_target_pairs={{1,0},{2,1},{3,2},{5,4},{6,5},{7,6},{9,8},{10,9},{11,10},{13,12},{... | collective-permute-start | bytes 15368 | tf_op jit(solution)/shard_map/ppermute | solution.py:30
  92.6 12.6 %collective-permute-start.4 = (f32[80,2,256]{2,0,1:T(8,128)S(1)}, f32[80,2,256]{2,0,1:T(8,128)S(1)}, u32[]{:S(2)}, u32[]{:S(2)}) collective-permute-start(f32[80,2,256]{2,0,1:T(8,128)S(1)} %slice.555), channel_id=1, source_target_pairs={{0,252},{4,0},{8,4},{12,8},{16,12},{20,16},{24,20},{28,24},{32,28}... | collective-permute-start | bytes 491528 | tf_op jit(solution)/shard_map/ppermute | solution.py:24
  103.0 46.2 %copy-start.10 = (f32[80,4,256]{2,0,1:T(8,128)}, f32[80,4,256]{2,0,1:T(8,128)S(1)}, u32[]{:S(2)}) copy-start(f32[80,4,256]{2,0,1:T(8,128)S(1)} %get-tuple-element.39) | copy-start | bytes 983044
  105.5 8.1 %collective-permute-start.5 = (f32[2,80,2,2]{3,1,2,0:T(8,128)S(1)}, f32[2,80,2,2]{3,1,2,0:T(8,128)S(1)}, u32[]{:S(2)}, u32[]{:S(2)}) collective-permute-start(f32[2,80,2,2]{3,1,2,0:T(8,128)S(1)} %pad_maximum_fusion.13), channel_id=1, source_target_pairs={{1,0},{2,1},{3,2},{5,4},{6,5},{7,6},{9,8},{10,9},{11,10},{13,12},{... | collective-permute-start | bytes 7688 | tf_op jit(solution)/shard_map/ppermute | solution.py:30
  107.5 44.5 %copy-start.8 = (f32[80,4,256]{2,0,1:T(8,128)}, f32[80,4,256]{2,0,1:T(8,128)S(1)}, u32[]{:S(2)}) copy-start(f32[80,4,256]{2,0,1:T(8,128)S(1)} %get-tuple-element.41) | copy-start | bytes 983044
  114.1 7.7 %collective-permute-start.6 = (f32[80,2,128]{2,0,1:T(8,128)S(1)}, f32[80,2,128]{2,0,1:T(8,128)S(1)}, u32[]{:S(2)}, u32[]{:S(2)}) collective-permute-start(f32[80,2,128]{2,0,1:T(8,128)S(1)} %get-tuple-element.62), channel_id=1, source_target_pairs={{0,252},{4,0},{8,4},{12,8},{16,12},{20,16},{24,20},{28,24},{32,28}... | collective-permute-start | bytes 245768 | tf_op jit(solution)/shard_map/ppermute | solution.py:24
  122.1 6.4 %collective-permute-start.7 = (f32[2,80,1,2]{1,3,2,0:T(2,128)S(1)}, f32[2,80,1,2]{1,3,2,0:T(2,128)S(1)}, u32[]{:S(2)}, u32[]{:S(2)}) collective-permute-start(f32[2,80,1,2]{1,3,2,0:T(2,128)S(1)} %pad_maximum_fusion.29), channel_id=1, source_target_pairs={{1,0},{2,1},{3,2},{5,4},{6,5},{7,6},{9,8},{10,9},{11,10},{13,12},{... | collective-permute-start | bytes 3848 | tf_op jit(solution)/shard_map/ppermute | solution.py:30
  130.2 3.1 %collective-permute-start.8 = (f32[4,80,1,1]{1,3,2,0:T(1,128)S(1)}, f32[4,80,1,1]{1,3,2,0:T(1,128)S(1)}, u32[]{:S(2)}, u32[]{:S(2)}) collective-permute-start(f32[4,80,1,1]{1,3,2,0:T(1,128)S(1)} %pad_maximum_fusion.30), channel_id=1, source_target_pairs={{0,1},{1,2},{2,3},{4,5},{5,6},{6,7},{8,9},{9,10},{10,11},{12,13},{... | collective-permute-start | bytes 3848 | tf_op jit(solution)/shard_map/ppermute | solution.py:30
  134.3 8.8 %collective-permute-start.9 = (f32[2,80,1,128]{3,1,2,0:T(8,128)S(1)}, f32[2,80,1,128]{3,1,2,0:T(8,128)S(1)}, u32[]{:S(2)}, u32[]{:S(2)}) collective-permute-start(f32[2,80,1,128]{3,1,2,0:T(8,128)S(1)} %pad_maximum_fusion.18), channel_id=1, source_target_pairs={{0,4},{4,8},{8,12},{12,16},{16,20},{20,24},{24,28},{28,32},{32,36}... | collective-permute-start | bytes 245768 | tf_op jit(solution)/shard_map/ppermute | solution.py:24
  143.3 6.7 %collective-permute-start.10 = (f32[4,80,2,1]{1,2,3,0:T(2,128)S(1)}, f32[4,80,2,1]{1,2,3,0:T(2,128)S(1)}, u32[]{:S(2)}, u32[]{:S(2)}) collective-permute-start(f32[4,80,2,1]{1,2,3,0:T(2,128)S(1)} %pad_maximum_fusion.28), channel_id=1, source_target_pairs={{0,1},{1,2},{2,3},{4,5},{5,6},{6,7},{8,9},{9,10},{10,11},{12,13},{... | collective-permute-start | bytes 7688 | tf_op jit(solution)/shard_map/ppermute | solution.py:30
  151.6 8.5 %collective-permute-start.11 = (f32[2,80,1,256]{3,1,2,0:T(8,128)S(1)}, f32[2,80,1,256]{3,1,2,0:T(8,128)S(1)}, u32[]{:S(2)}, u32[]{:S(2)}) collective-permute-start(f32[2,80,1,256]{3,1,2,0:T(8,128)S(1)} %pad_maximum_fusion.15), channel_id=1, source_target_pairs={{0,4},{4,8},{8,12},{12,16},{16,20},{20,24},{24,28},{28,32},{32,36}... | collective-permute-start | bytes 491528 | tf_op jit(solution)/shard_map/ppermute | solution.py:24
  160.2 13.3 %copy-start.9 = (f32[80,4,256]{2,0,1:T(8,128)S(1)}, f32[80,4,256]{2,0,1:T(8,128)}, u32[]{:S(2)}) copy-start(f32[80,4,256]{2,0,1:T(8,128)} %copy-done.8) | copy-start | bytes 983044
  160.5 7.9 %collective-permute-start.12 = (f32[4,80,4,1]{1,2,3,0:T(4,128)S(1)}, f32[4,80,4,1]{1,2,3,0:T(4,128)S(1)}, u32[]{:S(2)}, u32[]{:S(2)}) collective-permute-start(f32[4,80,4,1]{1,2,3,0:T(4,128)S(1)} %pad_maximum_fusion.27), channel_id=1, source_target_pairs={{0,1},{1,2},{2,3},{4,5},{5,6},{6,7},{8,9},{9,10},{10,11},{12,13},{... | collective-permute-start | bytes 15368 | tf_op jit(solution)/shard_map/ppermute | solution.py:30
  177.0 13.9 %copy-start.5 = (f32[80,4,512]{2,0,1:T(8,128)}, f32[80,4,512]{2,0,1:T(8,128)S(1)}, u32[]{:S(2)}) copy-start(f32[80,4,512]{2,0,1:T(8,128)S(1)} %fusion.20) | copy-start | bytes 1966084
  177.9 21.7 %collective-permute-start.13 = (f32[2,80,1,512]{3,1,2,0:T(8,128)}, f32[2,80,1,512]{3,1,2,0:T(8,128)}, u32[]{:S(2)}, u32[]{:S(2)}) collective-permute-start(f32[2,80,1,512]{3,1,2,0:T(8,128)} %pad_maximum_fusion.12), channel_id=1, source_target_pairs={{0,4},{4,8},{8,12},{12,16},{16,20},{20,24},{24,28},{28,32},{32,36}... | collective-permute-start | bytes 983048 | tf_op jit(solution)/shard_map/ppermute | solution.py:24
  192.4 18.5 %copy-start.2 = (f32[80,8,512]{2,1,0:T(8,128)}, f32[80,8,512]{2,1,0:T(8,128)S(1)}, u32[]{:S(2)}) copy-start(f32[80,8,512]{2,1,0:T(8,128)S(1)} %get-tuple-element.29) | copy-start | bytes 3932164
  201.9 10.8 %collective-permute-start.14 = (f32[4,80,8,1]{1,2,3,0:T(8,128)S(1)}, f32[4,80,8,1]{1,2,3,0:T(8,128)S(1)}, u32[]{:S(2)}, u32[]{:S(2)}) collective-permute-start(f32[4,80,8,1]{1,2,3,0:T(8,128)S(1)} %pad_maximum_fusion.26), channel_id=1, source_target_pairs={{0,1},{1,2},{2,3},{4,5},{5,6},{6,7},{8,9},{9,10},{10,11},{12,13},{... | collective-permute-start | bytes 30728 | tf_op jit(solution)/shard_map/ppermute | solution.py:30
  237.1 14.0 %copy-start.7 = (f32[1,80,1,1024]{3,2,1,0:T(1,128)S(1)}, f32[1,80,1,1024]{3,2,1,0:T(1,128)}, u32[]{:S(2)}) copy-start(f32[1,80,1,1024]{3,2,1,0:T(1,128)} %slice_bitcast_fusion.5) | copy-start | bytes 983044
  251.8 18.5 %collective-permute-start.15 = (f32[2,80,1,1024]{3,2,1,0:T(1,128)S(1)}, f32[2,80,1,1024]{3,2,1,0:T(1,128)S(1)}, u32[]{:S(2)}, u32[]{:S(2)}) collective-permute-start(f32[2,80,1,1024]{3,2,1,0:T(1,128)S(1)} %pad_maximum_fusion.8), channel_id=1, source_target_pairs={{0,4},{4,8},{8,12},{12,16},{16,20},{20,24},{24,28},{28,32},{32,36}... | collective-permute-start | bytes 1966088 | tf_op jit(solution)/shard_map/ppermute | solution.py:24
  (6 other events, 21.4 us)
where the time goes:
time: 287 us; the launch traced here: 283 us
  matrix products  68.3 us (24%)
  starting transfers between devices  62.2 us (22%)
  waiting for transfers between devices  61.4 us (21%)
  local copies, waits for them, and re-layouts  57.6 us (20%)
  other arithmetic  31.5 us (11%)
    dot_general x16, matrix products, lat_apply(): jnp.einsum('mcr,rk->mck', field, matrix, precision=lax.Precision.HIGHEST)  68.3 us
    ppermute x8, waiting for transfers between devices, from_behind(): return lax.ppermute(x, axis, [(i, (i + by) % size) for i in range(size)])  39.5 us
    ppermute x8, starting transfers between devices, from_behind(): return lax.ppermute(x, axis, [(i, (i + by) % size) for i in range(size)])  32.9 us
    ppermute x8, starting transfers between devices, passed_along(): return lax.ppermute(x, axis, pairs)  29.3 us
    ppermute x8, waiting for transfers between devices, passed_along(): return lax.ppermute(x, axis, pairs)  21.9 us
    unnamed x31, local copies, waits for them, and re-layouts  10.8 us
    add x8, other arithmetic, tap_matrix(): result = result + taps[tap] * (offset == tap).astype(jnp.float32)  9.07 us
    concatenate x2, local copies, waits for them, and re-layouts, lat_join_ext(): return lat_apply(jnp.concatenate([low_ext, high_ext], 2), matrix)  8.92 us
  transfers between devices with their start and end apart: 16, of which 12 were waited for; matrix products, arithmetic and copies ran while one was open for 17% of the time, Pallas kernels for 0%

commit v1 on v0

v1 whole, which is shorter than its diff:
```python
import math

import jax
import jax.numpy as jnp
from jax import lax
from jax.experimental import pallas as pl
from jax.experimental.pallas import tpu as pltpu
from jax.sharding import PartitionSpec as P

F32 = jnp.float32
LANES = 128
M = 16
LON = 16
HALO = 32
Q = math.sqrt(3.0)
R = 2.0 - Q
H0 = (1.0 + Q) / (4.0 * math.sqrt(2.0))
MESH = pl.DeviceIdType.MESH
MAIN = (8, 4, 2, 1)
USED = (2 * HALO, HALO, HALO // 2, HALO // 4)
OFFSETS = (0, 2, 4, 6, 8, 10)

GATHER = lax.GatherDimensionNumbers(
    offset_dims=(),
    collapsed_slice_dims=(1,),
    start_index_map=(1,),
    operand_batching_dims=(0,),
    start_indices_batching_dims=(0,),
)


def lane_ids(rows):
    return lax.broadcasted_iota(jnp.int32, (rows, LANES), 1)


def permute(x, index):
    return lax.gather(
        x, index[..., None], GATHER, (1, 1), mode=lax.GatherScatterMode.PROMISE_IN_BOUNDS
    )


def roll(x, by):
    by = by % LANES
    return x if by == 0 else pltpu.roll(x, by, 1)


def patterns(rows):
    lane = lane_ids(rows)
    front = lane < 64
    half = lane & 63
    even_odd = 2 * half + jnp.where(front, 0, 1)
    odd_even = 2 * half + jnp.where(front, 1, 0)
    pair = lane >> 1
    odd = lane & 1
    join_front = pair + 64 * odd
    join_back = pair + 64 - 64 * odd
    return lane, front, even_odd, odd_even, join_front, join_back


def split_pair(a, b, pat):
    _, front, even_odd, odd_even, _, _ = pat
    pa = permute(a, even_odd)
    if b is None:
        return pa, roll(pa, 64)
    pb = permute(b, odd_even)
    return jnp.where(front, pa, pb), roll(jnp.where(front, pb, pa), 64)


def join_pair(even, odd, pat, both=True):
    _, front, _, _, join_front, join_back = pat
    turned = roll(odd, 64)
    a = permute(jnp.where(front, even, turned), join_front)
    if not both:
        return [a]
    return [a, permute(jnp.where(front, turned, even), join_back)]


def shift_left(tiles, used, pat):
    lane = pat[0]
    if len(tiles) == 1:
        t = tiles[0]
        last = 64 + used - 1
        return [jnp.where(lane == last, roll(t, last), roll(t, -1))]
    turned = [roll(t, -1) for t in tiles]
    shifted = [
        jnp.where(lane == LANES - 1, turned[b + 1], turned[b]) for b in range(len(tiles) - 1)
    ]
    shifted.append(jnp.where(lane == used - 1, roll(tiles[0], used - 1), turned[-1]))
    return shifted


def shift_right(tiles, used, pat):
    lane = pat[0]
    first = lane == 0
    if len(tiles) == 1:
        t = tiles[0]
        last = 64 + used - 1
        return [jnp.where(first, roll(t, -last), roll(t, 1))]
    turned = [roll(t, 1) for t in tiles[:-1]]
    shifted = [jnp.where(first, roll(tiles[-1], -(used - 1)), turned[0])]
    for b in range(1, len(tiles) - 1):
        shifted.append(jnp.where(first, turned[b - 1], turned[b]))
    shifted.append(jnp.where(first, turned[-1], roll(tiles[-1], 1)))
    return shifted


def lat_split(level, tiles, pat):
    main = MAIN[level]
    if level < 3:
        pairs = [split_pair(tiles[2 * b], tiles[2 * b + 1], pat) for b in range(main // 2)]
        pairs.append(split_pair(tiles[main], None, pat))
    else:
        pairs = [split_pair(tiles[0], tiles[1], pat)]
    u = [e + Q * o for e, o in pairs]
    t = shift_left([Q * e - o for e, o in pairs], USED[level] // 2, pat)
    low = [a + R * b for a, b in zip(u, t)]
    high = [b - R * a for a, b in zip(u, t)]
    return low, high


def lat_join(level, low, high, pat):
    main = MAIN[level]
    u = [a - R * b for a, b in zip(low, high)]
    t = shift_right([R * a + b for a, b in zip(low, high)], USED[level] // 2, pat)
    pairs = [(a + Q * b, Q * a - b) for a, b in zip(u, t)]
    if level == 3:
        return join_pair(*pairs[0], pat)
    tiles = []
    for b in range(main // 2):
        tiles += join_pair(*pairs[b], pat)
    if level > 0:
        tiles += join_pair(*pairs[-1], pat, both=False)
    return tiles


def tiles_of(x):
    return [x[:, LANES * b : LANES * (b + 1)] for b in range(x.shape[1] // LANES)]


def wide(tiles):
    return tiles[0] if len(tiles) == 1 else jnp.concatenate(tiles, 1)


def stack(a, b):
    return [jnp.concatenate([x, y], 0) for x, y in zip(a, b)]


def kernel(
    x_hbm, table, band_index, out_hbm,
    xin, xh, oxt, u0, u1, u2, u3, ul,
    c1, c2, c3, g0, g1, g2, b0, b1, b2,
    wh0, wh1, wh2, wh3, wb0, wb1, wb2, wb3, wc,
    tab0, tab1, tab2, tab3, side,
    hl_s, hl_r, hr_s, hr_r, ma_s, ma_r, mb_s, mb_r, mc_s, mc_r, md_s, md_r,
    in_sem, out_sem, send, recv, side_send, side_recv,
):
    chunks = xin.shape[0]
    lon, lat = lax.axis_index("lon"), lax.axis_index("lat")
    lons, lats = lax.axis_size("lon"), lax.axis_size("lat")
    nxt, prv = (lax.rem(lon + 1, lons), lat), (lax.rem(lon + lons - 1, lons), lat)
    right, left = (lon, lat + 1), (lon, lat - 1)
    has_right, has_left = lat < lats - 1, lat > 0

    def load(c, i):
        return pltpu.make_async_copy(
            x_hbm.at[pl.ds(M * c, M), i], xin.at[c, i], in_sem.at[c]
        )

    def store(c, i):
        return pltpu.make_async_copy(
            oxt.at[c, i], out_hbm.at[pl.ds(M * c, M), i], out_sem.at[c]
        )

    def send_to(kind, c, src, dst, to):
        return pltpu.make_async_remote_copy(
            src_ref=src.at[c], dst_ref=dst.at[c],
            send_sem=send.at[kind, c], recv_sem=recv.at[kind, c],
            device_id=to, device_id_type=MESH,
        )

    def begin(c, carry):
        for i in range(LON):
            load(c, i).start()
        return carry

    lax.fori_loop(0, chunks, begin, 0)

    barrier = pltpu.get_barrier_semaphore()
    for to in (nxt, prv):
        pl.semaphore_signal(barrier, inc=1, device_id=to, device_id_type=MESH)

    @pl.when(has_left)
    def _():
        pl.semaphore_signal(barrier, inc=1, device_id=left, device_id_type=MESH)

    @pl.when(has_right)
    def _():
        pl.semaphore_signal(barrier, inc=1, device_id=right, device_id_type=MESH)

    peers = 2 + jnp.where(has_left, 1, 0) + jnp.where(has_right, 1, 0)
    pl.semaphore_wait(barrier, peers)

    last_tile = pl.ds(table.shape[1] - LANES, LANES)

    def side_copy():
        return pltpu.make_async_remote_copy(
            src_ref=table.at[:, last_tile], dst_ref=side,
            send_sem=side_send, recv_sem=side_recv,
            device_id=right, device_id_type=MESH,
        )

    @pl.when(has_right)
    def _():
        side_copy().start()

    def stage_z(c):
        pltpu.make_async_copy(x_hbm.at[pl.ds(M * c, M)], xin.at[c], in_sem.at[c]).wait()
        quarter = lane_ids(M) >> 5
        for k in range(LON // 4):
            to_left = to_right = None
            for n in range(4):
                head = roll(xin[c, 4 * k + n, :, :LANES], HALO * n)
                tail = roll(xin[c, 4 * k + n, :, 7 * LANES :], HALO * (n + 1))
                to_left = head if n == 0 else jnp.where(quarter == n, head, to_left)
                to_right = tail if n == 0 else jnp.where(quarter == n, tail, to_right)
            hr_s[c, k] = to_left
            hl_s[c, k] = to_right

        @pl.when(has_left)
        def _():
            send_to(0, c, hr_s, hr_r, left).start()

        @pl.when(has_right)
        def _():
            send_to(1, c, hl_s, hl_r, right).start()

    def keep(level, p, c, low, high, coarse, bands, highs, wb, wh):
        coarse[c, p] = wide([x[:M] for x in low])
        bands[c, p] = wide([x[M:] for x in low]) * wb[...]
        highs[c, p] = wide(high) * wh[...]

    def field(ref, c, i):
        return tiles_of(ref[c, i])

    def first(e, o):
        return [a + Q * b for a, b in zip(e, o)]

    def second(e, o):
        return [Q * a - b for a, b in zip(e, o)]

    def lon_split(u, t):
        return stack([a + R * b for a, b in zip(u, t)], [b - R * a for a, b in zip(u, t)])

    def lon_join(tiles):
        lo, hi = [x[:M] for x in tiles], [x[M:] for x in tiles]
        return [a - R * b for a, b in zip(lo, hi)], [R * a + b for a, b in zip(lo, hi)]

    def input_field(c, i):
        return tiles_of(xin[c, i]) + [xh[c, i]]

    def stage_a(c):
        @pl.when(has_right)
        def _():
            send_to(0, c, hr_s, hr_r, left).wait_recv()

        @pl.when(has_left)
        def _():
            send_to(1, c, hl_s, hl_r, right).wait_recv()

        pat = patterns(2 * M)
        lane = lane_ids(M)
        in_right = (lane < HALO) & has_right
        in_left = (lane >= HALO) & (lane < 2 * HALO) & has_left
        for i in range(LON):
            k, n = i // 4, i % 4
            r_part = roll(hr_r[c, k], -HALO * n)
            l_part = roll(hl_r[c, k], HALO * (1 - n))
            xh[c, i] = jnp.where(in_right, r_part, jnp.where(in_left, l_part, 0.0))

        x0, x1 = input_field(c, 0), input_field(c, 1)
        t0 = second(x0, x1)
        u = first(x0, x1)
        for p in range(7):
            x0, x1 = input_field(c, 2 * p + 2), input_field(c, 2 * p + 3)
            low, high = lat_split(0, lon_split(u, second(x0, x1)), pat)
            keep(0, p, c, low, high, c1, b0, g0, wb0, wh0)
            u = first(x0, x1)
        u0[c] = wide(u)

        t1 = second(field(c1, c, 0), field(c1, c, 1))
        for p in range(2):
            u = first(field(c1, c, 2 * p), field(c1, c, 2 * p + 1))
            t = second(field(c1, c, 2 * p + 2), field(c1, c, 2 * p + 3))
            low, high = lat_split(1, lon_split(u, t), pat)
            keep(1, p, c, low, high, c2, b1, g1, wb1, wh1)
        t2 = second(field(c2, c, 0), field(c2, c, 1))
        halo = jnp.where(lane < 64, t0[8], jnp.where(lane < 96, roll(t1[4], 64), roll(t2[2], 96)))
        ma_s[c] = wide(t0[:8] + t1[:4] + t2[:2] + [halo])
        send_to(2, c, ma_s, ma_r, prv).start()

    def stage_b(c):
        send_to(2, c, ma_s, ma_r, prv).wait_recv()
        pat = patterns(2 * M)
        got = tiles_of(ma_r[c])
        halo = got[14]
        t0, t1, t2 = got[:8] + [halo], got[8:12] + [roll(halo, -64)], got[12:14] + [roll(halo, -96)]
        low, high = lat_split(0, lon_split(tiles_of(u0[c]), t0), pat)
        keep(0, 7, c, low, high, c1, b0, g0, wb0, wh0)
        for p in (2, 3):
            u = first(field(c1, c, 2 * p), field(c1, c, 2 * p + 1))
            t = second(field(c1, c, 6), field(c1, c, 7)) if p == 2 else t1
            low, high = lat_split(1, lon_split(u, t), pat)
            keep(1, p, c, low, high, c2, b1, g1, wb1, wh1)
        for p in (0, 1):
            u = first(field(c2, c, 2 * p), field(c2, c, 2 * p + 1))
            t = second(field(c2, c, 2), field(c2, c, 3)) if p == 0 else t2
            low, high = lat_split(2, lon_split(u, t), pat)
            keep(2, p, c, low, high, c3, b2, g2, wb2, wh2)
        mb_s[c] = wide(second(field(c3, c, 0), field(c3, c, 1)))
        send_to(3, c, mb_s, mb_r, prv).start()

    def stage_c(c):
        send_to(3, c, mb_s, mb_r, prv).wait_recv()
        pat = patterns(2 * M)
        u = first(field(c3, c, 0), field(c3, c, 1))
        low, high = lat_split(3, lon_split(u, tiles_of(mb_r[c])), pat)
        low = [low[0] * wc[...]]
        high = [high[0] * wh3[...]]
        u, t = lon_join(lat_join(3, low, high, pat))
        u3[c] = wide(u)
        mc_s[c] = wide(t)
        send_to(4, c, mc_s, mc_r, nxt).start()

    def synthesis(level, c, p, coarse, bands, highs, pat):
        return lon_join(
            lat_join(level, stack(field(coarse, c, p), field(bands, c, p)), field(highs, c, p), pat)
        )

    def put(ref, c, p, u, t):
        ref[c, 2 * p] = wide(first(u, t))
        ref[c, 2 * p + 1] = wide(second(u, t))

    def stage_d(c):
        send_to(4, c, mc_s, mc_r, nxt).wait_recv()
        pat = patterns(2 * M)
        lane = lane_ids(M)
        put(c3, c, 0, tiles_of(u3[c]), tiles_of(mc_r[c]))
        u, t_two = synthesis(2, c, 0, c3, b2, g2, pat)
        u2[c] = wide(u)
        u, t2 = synthesis(2, c, 1, c3, b2, g2, pat)
        put(c2, c, 1, u, t_two)
        u, t_one = synthesis(1, c, 2, c2, b1, g1, pat)
        u1[c] = wide(u)
        u, t1 = synthesis(1, c, 3, c2, b1, g1, pat)
        put(c1, c, 3, u, t_one)
        u, t0 = synthesis(0, c, 7, c1, b0, g0, pat)
        ul[c] = wide(u)
        halo = jnp.where(lane < 64, t1[4], roll(t2[2], 64))
        md_s[c] = wide(t0 + t1[:4] + t2[:2] + [halo])
        send_to(5, c, md_s, md_r, nxt).start()

    def stage_e(c):
        send_to(5, c, md_s, md_r, nxt).wait_recv()
        pat = patterns(2 * M)
        got = tiles_of(md_r[c])
        halo = got[14]
        t0, t1, t2 = got[:8], got[8:12] + [halo], got[12:14] + [roll(halo, -64)]
        put(c2, c, 0, tiles_of(u2[c]), t2)
        t = t1
        for p in (0, 1):
            u, t_next = synthesis(1, c, p, c2, b1, g1, pat)
            put(c1, c, p, u, t)
            t = t_next
        put(c1, c, 2, tiles_of(u1[c]), t)
        t = t0
        for p in range(7):
            u, t_next = synthesis(0, c, p, c1, b0, g0, pat)
            put(oxt, c, p, u, t)
            t = t_next
        put(oxt, c, 7, tiles_of(ul[c]), t)
        for i in range(LON):
            store(c, i).start()

    def weights():
        @pl.when(has_right)
        def _():
            side_copy().wait_send()

        @pl.when(has_left)
        def _():
            side_copy().wait_recv()

        pat = patterns(TABLE_ROWS)
        lane, front, even_odd, odd_even, _, _ = pat

        def halved(tiles):
            if len(tiles) == 1:
                return [permute(tiles[0], even_odd)]
            return [
                jnp.where(front, permute(a, even_odd), permute(b, odd_even))
                for a, b in zip(tiles[::2], tiles[1::2])
            ]

        def between(x, lo, hi):
            return jnp.where((lane >= lo) & (lane < hi) & has_left, x, 0.0)

        main, edge = tiles_of(table[...]), side[...]
        tab0[...] = wide(main + [between(roll(edge, 32), 16, 32)]) * H0**4
        main, edge = halved(main), permute(edge, even_odd)
        tab1[...] = wide(main + [between(roll(edge, 80), 8, 16)]) * H0**8
        main, edge = halved(main), permute(edge, even_odd)
        tab2[...] = wide(main + [between(roll(edge, 104), 4, 8)]) * H0**12
        main, edge = halved(main), permute(edge, even_odd)
        tab3[...] = jnp.where(lane < 64, main[0], between(roll(edge, 52), 66, 68)) * H0**16

        def row(tab, i):
            one = tab[pl.ds(band_index[i], 1), :]
            return jnp.broadcast_to(one, (M, one.shape[1]))

        for level, (tab, wh, wb) in enumerate(
            ((tab0, wh0, wb0), (tab1, wh1, wb1), (tab2, wh2, wb2), (tab3, wh3, wb3))
        ):
            wh[:M] = row(tab, 3 * level)
            wh[M:] = row(tab, 3 * level + 2)
            wb[...] = row(tab, 3 * level + 1)
        wc[:M] = row(tab3, 12)
        wc[M:] = wb3[...]

    lax.fori_loop(0, OFFSETS[1], lambda c, carry: (stage_z(c), carry)[1], 0)
    weights()

    def step(s, carry):
        for stage, offset in zip((stage_z, stage_a, stage_b, stage_c, stage_d, stage_e), OFFSETS):
            c = s - offset

            @pl.when((c >= 0) & (c < chunks))
            def _(stage=stage, c=c):
                stage(c)

        return carry

    lax.fori_loop(OFFSETS[1], chunks + OFFSETS[-1], step, 0)

    def finish(c, carry):
        @pl.when(has_left)
        def _():
            send_to(0, c, hr_s, hr_r, left).wait_send()

        @pl.when(has_right)
        def _():
            send_to(1, c, hl_s, hl_r, right).wait_send()

        send_to(2, c, ma_s, ma_r, prv).wait_send()
        send_to(3, c, mb_s, mb_r, prv).wait_send()
        send_to(4, c, mc_s, mc_r, nxt).wait_send()
        send_to(5, c, md_s, md_r, nxt).wait_send()
        pltpu.make_async_copy(oxt.at[c], out_hbm.at[pl.ds(M * c, M)], out_sem.at[c]).wait()
        return carry

    lax.fori_loop(0, chunks, finish, 0)


TABLE_ROWS = 8


def per_device(perturbation, weight_table, band_index):
    members = perturbation.shape[0]
    chunks = members // M
    width = perturbation.shape[2]
    widths = [(m + 1) * LANES for m in MAIN]
    halves = [widths[1], widths[2], widths[3], LANES]

    def vmem(*shape):
        return pltpu.VMEM(shape, F32)

    per = [
        vmem(chunks, LON, M, width), vmem(chunks, LON, M, LANES), vmem(chunks, LON, M, width),
        vmem(chunks, M, widths[0]), vmem(chunks, M, widths[1]), vmem(chunks, M, widths[2]),
        vmem(chunks, M, widths[3]), vmem(chunks, M, width),
        vmem(chunks, 8, M, widths[1]), vmem(chunks, 4, M, widths[2]), vmem(chunks, 2, M, widths[3]),
        vmem(chunks, 8, 2 * M, halves[0]), vmem(chunks, 4, 2 * M, halves[1]),
        vmem(chunks, 2, 2 * M, halves[2]),
        vmem(chunks, 8, M, halves[0]), vmem(chunks, 4, M, halves[1]), vmem(chunks, 2, M, halves[2]),
    ]
    weights = [vmem(2 * M, h) for h in halves] + [vmem(M, h) for h in halves] + [vmem(2 * M, LANES)]
    tables = [vmem(TABLE_ROWS, h) for h in halves] + [vmem(TABLE_ROWS, LANES)]
    messages = [vmem(chunks, LON // 4, M, LANES)] * 4
    messages += [vmem(chunks, M, 15 * LANES)] * 2 + [vmem(chunks, M, 2 * LANES)] * 4
    messages += [vmem(chunks, M, 15 * LANES)] * 2
    dma = pltpu.SemaphoreType.DMA
    return pl.pallas_call(
        kernel,
        out_shape=jax.ShapeDtypeStruct(perturbation.shape, F32),
        in_specs=[
            pl.BlockSpec(memory_space=pl.ANY),
            pl.BlockSpec(memory_space=pltpu.VMEM),
            pl.BlockSpec(memory_space=pltpu.SMEM),
        ],
        out_specs=pl.BlockSpec(memory_space=pl.ANY),
        scratch_shapes=per + weights + tables + messages
        + [dma((chunks,)), dma((chunks,)), dma((6, chunks)), dma((6, chunks)), dma, dma],
        compiler_params=pltpu.CompilerParams(
            collective_id=0, has_side_effects=True, vmem_limit_bytes=60 * 2**20
        ),
    )(perturbation, weight_table, band_index)


def solution(mesh):
    placed = (P(None, "lon", "lat"), P(None, "lat"), P())
    return jax.shard_map(
        per_device, mesh=mesh, in_specs=placed, out_specs=P(None, "lon", "lat"), check_vma=False
    )
```

time: 287 us -> 74 us (0.26); the launches traced: 283 us -> 73.8 us
  matrix products: 68.3 us -> 0 us
  Pallas kernels: 0 us -> 68.1 us
  starting transfers between devices: 62.2 us -> 0 us
  waiting for transfers between devices: 61.4 us -> 0 us
  local copies, waits for them, and re-layouts: 57.6 us -> 5.7 us
  other arithmetic: 31.5 us -> 0 us
    dot_general x16 -> x0, matrix products: 68.3 us -> none  [lat_apply(): jnp.einsum('mcr,rk->mck', field, matrix, precision=lax.Precision.HIGHEST)]
    pallas_call x0 -> x1, Pallas kernels: none -> 68.1 us  [per_device(): pl.pallas_call(kernel, out_shape=jax.ShapeDtypeStruct(perturbation.shape,...]
    ppermute x16 -> x0, starting transfers between devices: 62.2 us -> none  [the longest x8 32.9 us: from_behind(): return lax.ppermute(x, axis, [(i, (i + by) % size) for i in range(size)])]
    ppermute x16 -> x0, waiting for transfers between devices: 61.4 us -> none  [the longest x8 39.5 us: from_behind(): return lax.ppermute(x, axis, [(i, (i + by) % size) for i in range(size)])]
    slice x33 -> x0, local copies, waits for them, and re-layouts: 14.6 us -> none  [the longest x5 3.76 us: join_lat(): bands[1][:, :, -1:]]
    add x12 -> x0, other arithmetic: 12.3 us -> none  [the longest x8 9.07 us: tap_matrix(): result = result + taps[tap] * (offset == tap).astype(jnp.float32)]
    concatenate x3 -> x0, local copies, waits for them, and re-layouts: 9.88 us -> none  [the longest x2 8.92 us: lat_join_ext(): return lat_apply(jnp.concatenate([low_ext, high_ext], 2), matrix)]
    squeeze x29 -> x0, local copies, waits for them, and re-layouts: 9.02 us -> none  [the longest x1 3.71 us: lon_split(): odd = pairs[:, :, 1]]
  transfers between devices with their start and end apart: 16 -> 0, of which waited for: 12 -> 0; matrix products, arithmetic and copies ran while one was open for 17% -> 0% of each run, Pallas kernels for 0% -> 0%
where the time goes in v1:
time: 74 us; the launch traced here: 73.8 us
  Pallas kernels  68.1 us (92%)
  local copies, waits for them, and re-layouts  5.7 us (8%)
    pallas_call x1, Pallas kernels, per_device(): pl.pallas_call(kernel, out_shape=jax.ShapeDtypeStruct(perturbation.shape,...  68.1 us
    unnamed x1, local copies, waits for them, and re-layouts  5.7 us

profile of v1, /device:TPU:1, one launch (start us, length us, event | category | flops | bytes accessed | tf_op | source)
XLA Modules:
  0.0 73.8 jit_solution(2311374520816388583)
XLA Ops:
  0.0 68.1 %shard_map.37 = f32[80,16,1024]{2,1,0:T(8,128)} custom-call(f32[80,16,1024]{2,1,0:T(8,128)} %x_hbm.1, f32[8,512]{1,0:T(8,128)} %table.1, s32[13]{0:T(128)} %band_index.1), custom_call_target="tpu_custom_call" | custom-call | tf_op jit(solution)/shard_map/pallas_call | solution.py:491
  68.1 5.7 %copy.5 = f32[80,16,1024]{2,1,0:T(8,128)} copy(f32[80,16,1024]{2,1,0:T(8,128)} %shard_map.37) | data formatting | bytes 10485760

commit v2 on v1

--- a/solution.py
+++ b/solution.py
@@ -2,6 +2,7 @@
 
 import jax
 import jax.numpy as jnp
+import numpy as np
 from jax import lax
 from jax.experimental import pallas as pl
 from jax.experimental.pallas import tpu as pltpu
@@ -17,7 +18,6 @@
 H0 = (1.0 + Q) / (4.0 * math.sqrt(2.0))
 MESH = pl.DeviceIdType.MESH
 MAIN = (8, 4, 2, 1)
-USED = (2 * HALO, HALO, HALO // 2, HALO // 4)
 OFFSETS = (0, 2, 4, 6, 8, 10)
 
 GATHER = lax.GatherDimensionNumbers(
@@ -50,86 +50,64 @@
     half = lane & 63
     even_odd = 2 * half + jnp.where(front, 0, 1)
     odd_even = 2 * half + jnp.where(front, 1, 0)
-    pair = lane >> 1
-    odd = lane & 1
-    join_front = pair + 64 * odd
-    join_back = pair + 64 - 64 * odd
-    return lane, front, even_odd, odd_even, join_front, join_back
-
-
-def split_pair(a, b, pat):
-    _, front, even_odd, odd_even, _, _ = pat
-    pa = permute(a, even_odd)
-    if b is None:
-        return pa, roll(pa, 64)
-    pb = permute(b, odd_even)
-    return jnp.where(front, pa, pb), roll(jnp.where(front, pb, pa), 64)
-
-
-def join_pair(even, odd, pat, both=True):
-    _, front, _, _, join_front, join_back = pat
-    turned = roll(odd, 64)
-    a = permute(jnp.where(front, even, turned), join_front)
-    if not both:
-        return [a]
-    return [a, permute(jnp.where(front, turned, even), join_back)]
-
-
-def shift_left(tiles, used, pat):
-    lane = pat[0]
-    if len(tiles) == 1:
-        t = tiles[0]
-        last = 64 + used - 1
-        return [jnp.where(lane == last, roll(t, last), roll(t, -1))]
-    turned = [roll(t, -1) for t in tiles]
-    shifted = [
-        jnp.where(lane == LANES - 1, turned[b + 1], turned[b]) for b in range(len(tiles) - 1)
+    return lane, front, even_odd, odd_even
+
+
+def filter_matrices():
+    k = np.arange(LANES)
+    turned = (k + 1) % LANES
+    exact = np.zeros((2 * LANES, 2 * LANES), np.float64)
+    exact[2 * k, k], exact[2 * k + 1, k] = 1.0, Q
+    exact[2 * turned, LANES + k], exact[2 * turned + 1, LANES + k] = Q, -1.0
+    both = []
+    for matrix in (exact, exact.T):
+        head = matrix.astype(jnp.bfloat16)
+        rest = (matrix - head.astype(np.float64)).astype(jnp.bfloat16)
+        both.append(np.concatenate([head, head, rest], 0))
+    return np.stack(both)
+
+
+def multiply(blocks, matrix):
+    x = jnp.concatenate([wide(pair) for pair in blocks], 0)
+    head = x.astype(jnp.bfloat16)
+    rest = (x - head.astype(F32)).astype(jnp.bfloat16)
+    out = jnp.dot(
+        jnp.concatenate([head, rest, head], 1), matrix[...], preferred_element_type=F32
+    )
+    rows = blocks[0][0].shape[0]
+    return [
+        (out[rows * b : rows * (b + 1), :LANES], out[rows * b : rows * (b + 1), LANES:])
+        for b in range(len(blocks))
     ]
-    shifted.append(jnp.where(lane == used - 1, roll(tiles[0], used - 1), turned[-1]))
-    return shifted
-
-
-def shift_right(tiles, used, pat):
-    lane = pat[0]
-    first = lane == 0
-    if len(tiles) == 1:
-        t = tiles[0]
-        last = 64 + used - 1
-        return [jnp.where(first, roll(t, -last), roll(t, 1))]
-    turned = [roll(t, 1) for t in tiles[:-1]]
-    shifted = [jnp.where(first, roll(tiles[-1], -(used - 1)), turned[0])]
-    for b in range(1, len(tiles) - 1):
-        shifted.append(jnp.where(first, turned[b - 1], turned[b]))
-    shifted.append(jnp.where(first, turned[-1], roll(tiles[-1], 1)))
-    return shifted
-
-
-def lat_split(level, tiles, pat):
-    main = MAIN[level]
+
+
+def lat_split(level, tiles, matrix, last):
     if level < 3:
-        pairs = [split_pair(tiles[2 * b], tiles[2 * b + 1], pat) for b in range(main // 2)]
-        pairs.append(split_pair(tiles[main], None, pat))
+        main, halo = tiles[:-1], tiles[-1]
+        blocks = list(zip(main[::2], main[1::2])) + [(halo, halo)]
     else:
-        pairs = [split_pair(tiles[0], tiles[1], pat)]
-    u = [e + Q * o for e, o in pairs]
-    t = shift_left([Q * e - o for e, o in pairs], USED[level] // 2, pat)
+        blocks = [tuple(tiles)]
+    pairs = multiply(blocks, matrix)
+    u, t = [a for a, _ in pairs], [b for _, b in pairs]
+    if len(t) > 1:
+        t = [jnp.where(last, b, a) for a, b in zip(t, t[1:] + t[:1])]
     low = [a + R * b for a, b in zip(u, t)]
     high = [b - R * a for a, b in zip(u, t)]
     return low, high
 
 
-def lat_join(level, low, high, pat):
-    main = MAIN[level]
+def lat_join(level, low, high, matrix, last):
     u = [a - R * b for a, b in zip(low, high)]
-    t = shift_right([R * a + b for a, b in zip(low, high)], USED[level] // 2, pat)
-    pairs = [(a + Q * b, Q * a - b) for a, b in zip(u, t)]
-    if level == 3:
-        return join_pair(*pairs[0], pat)
-    tiles = []
-    for b in range(main // 2):
-        tiles += join_pair(*pairs[b], pat)
-    if level > 0:
-        tiles += join_pair(*pairs[-1], pat, both=False)
+    t = [R * a + b for a, b in zip(low, high)]
+    if len(t) > 1:
+        t = [jnp.where(last, b, a) for a, b in zip(t, t[-1:] + t[:-1])]
+    blocks = list(zip(u, t))
+    if level == 0:
+        blocks = blocks[:-1]
+    pairs = multiply(blocks, matrix)
+    tiles = [x for pair in pairs for x in pair]
+    if level in (1, 2):
+        del tiles[-2]
     return tiles
 
 
@@ -146,13 +124,13 @@
 
 
 def kernel(
-    x_hbm, table, band_index, out_hbm,
+    x_hbm, table, band_index, matrix_hbm, out_hbm,
     xin, xh, oxt, u0, u1, u2, u3, ul,
     c1, c2, c3, g0, g1, g2, b0, b1, b2,
     wh0, wh1, wh2, wh3, wb0, wb1, wb2, wb3, wc,
     tab0, tab1, tab2, tab3, side,
     hl_s, hl_r, hr_s, hr_r, ma_s, ma_r, mb_s, mb_r, mc_s, mc_r, md_s, md_r,
-    in_sem, out_sem, send, recv, side_send, side_recv,
+    matrices, in_sem, out_sem, send, recv, side_send, side_recv, matrix_sem,
 ):
     chunks = xin.shape[0]
     lon, lat = lax.axis_index("lon"), lax.axis_index("lat")
@@ -184,6 +162,9 @@
         return carry
 
     lax.fori_loop(0, chunks, begin, 0)
+    matrix_copy = pltpu.make_async_copy(matrix_hbm, matrices, matrix_sem)
+    matrix_copy.start()
+    forth, back = matrices.at[0], matrices.at[1]
 
     barrier = pltpu.get_barrier_semaphore()
     for to in (nxt, prv):
@@ -239,6 +220,14 @@
         bands[c, p] = wide([x[M:] for x in low]) * wb[...]
         highs[c, p] = wide(high) * wh[...]
 
+    def two(level, ps, c, pair, coarse, bands, highs, wb, wh):
+        last = lane_ids(4 * M) == LANES - 1
+        low, high = lat_split(level, stack(*pair), forth, last)
+        for n, p in enumerate(ps):
+            rows = slice(2 * M * n, 2 * M * (n + 1))
+            keep(level, p, c, [x[rows] for x in low], [x[rows] for x in high],
+                 coarse, bands, highs, wb, wh)
+
     def field(ref, c, i):
         return tiles_of(ref[c, i])
 
@@ -267,74 +256,87 @@
         def _():
             send_to(1, c, hl_s, hl_r, right).wait_recv()
 
-        pat = patterns(2 * M)
+        last = lane_ids(2 * M) == LANES - 1
         lane = lane_ids(M)
-        in_right = (lane < HALO) & has_right
-        in_left = (lane >= HALO) & (lane < 2 * HALO) & has_left
+        in_front = (lane < HALO) & has_right
+        in_right = (lane >= 64) & (lane < 96) & has_right
+        in_left = (lane >= 96) & has_left
         for i in range(LON):
             k, n = i // 4, i % 4
-            r_part = roll(hr_r[c, k], -HALO * n)
-            l_part = roll(hl_r[c, k], HALO * (1 - n))
-            xh[c, i] = jnp.where(in_right, r_part, jnp.where(in_left, l_part, 0.0))
+            r_part, l_part = hr_r[c, k], hl_r[c, k]
+            rest = jnp.where(in_left, roll(l_part, 96 - HALO * n), 0.0)
+            rest = jnp.where(in_right, roll(r_part, 64 - HALO * n), rest)
+            xh[c, i] = jnp.where(in_front, roll(r_part, -HALO * n), rest)
 
         x0, x1 = input_field(c, 0), input_field(c, 1)
         t0 = second(x0, x1)
         u = first(x0, x1)
         for p in range(7):
             x0, x1 = input_field(c, 2 * p + 2), input_field(c, 2 * p + 3)
-            low, high = lat_split(0, lon_split(u, second(x0, x1)), pat)
+            low, high = lat_split(0, lon_split(u, second(x0, x1)), forth, last)
             keep(0, p, c, low, high, c1, b0, g0, wb0, wh0)
             u = first(x0, x1)
         u0[c] = wide(u)
 
         t1 = second(field(c1, c, 0), field(c1, c, 1))
+        pair = []
         for p in range(2):
             u = first(field(c1, c, 2 * p), field(c1, c, 2 * p + 1))
             t = second(field(c1, c, 2 * p + 2), field(c1, c, 2 * p + 3))
-            low, high = lat_split(1, lon_split(u, t), pat)
-            keep(1, p, c, low, high, c2, b1, g1, wb1, wh1)
+            pair.append(lon_split(u, t))
+        two(1, (0, 1), c, pair, c2, b1, g1, wb1, wh1)
         t2 = second(field(c2, c, 0), field(c2, c, 1))
-        halo = jnp.where(lane < 64, t0[8], jnp.where(lane < 96, roll(t1[4], 64), roll(t2[2], 96)))
+        halo = jnp.where(lane < 32, roll(t2[2], 32), roll(t1[4], 64))
+        halo = jnp.where(lane < 64, halo, t0[8])
         ma_s[c] = wide(t0[:8] + t1[:4] + t2[:2] + [halo])
         send_to(2, c, ma_s, ma_r, prv).start()
 
     def stage_b(c):
         send_to(2, c, ma_s, ma_r, prv).wait_recv()
-        pat = patterns(2 * M)
+        last = lane_ids(2 * M) == LANES - 1
+        lane = lane_ids(M)
         got = tiles_of(ma_r[c])
         halo = got[14]
-        t0, t1, t2 = got[:8] + [halo], got[8:12] + [roll(halo, -64)], got[12:14] + [roll(halo, -96)]
-        low, high = lat_split(0, lon_split(tiles_of(u0[c]), t0), pat)
+        h0 = jnp.where(lane < 32, roll(halo, 64), halo)
+        h1 = jnp.where(lane < 64, roll(halo, 96), roll(halo, 64))
+        h2 = jnp.where(lane < 64, roll(halo, 112), roll(halo, 96))
+        t0, t1, t2 = got[:8] + [h0], got[8:12] + [h1], got[12:14] + [h2]
+        low, high = lat_split(0, lon_split(tiles_of(u0[c]), t0), forth, last)
         keep(0, 7, c, low, high, c1, b0, g0, wb0, wh0)
-        for p in (2, 3):
-            u = first(field(c1, c, 2 * p), field(c1, c, 2 * p + 1))
-            t = second(field(c1, c, 6), field(c1, c, 7)) if p == 2 else t1
-            low, high = lat_split(1, lon_split(u, t), pat)
-            keep(1, p, c, low, high, c2, b1, g1, wb1, wh1)
-        for p in (0, 1):
-            u = first(field(c2, c, 2 * p), field(c2, c, 2 * p + 1))
-            t = second(field(c2, c, 2), field(c2, c, 3)) if p == 0 else t2
-            low, high = lat_split(2, lon_split(u, t), pat)
-            keep(2, p, c, low, high, c3, b2, g2, wb2, wh2)
+        x0, x1 = field(c1, c, 6), field(c1, c, 7)
+        u = first(field(c1, c, 4), field(c1, c, 5))
+        pair = [lon_split(u, second(x0, x1)), lon_split(first(x0, x1), t1)]
+        two(1, (2, 3), c, pair, c2, b1, g1, wb1, wh1)
+        x0, x1 = field(c2, c, 2), field(c2, c, 3)
+        u = first(field(c2, c, 0), field(c2, c, 1))
+        pair = [lon_split(u, second(x0, x1)), lon_split(first(x0, x1), t2)]
+        two(2, (0, 1), c, pair, c3, b2, g2, wb2, wh2)
         mb_s[c] = wide(second(field(c3, c, 0), field(c3, c, 1)))
         send_to(3, c, mb_s, mb_r, prv).start()
 
     def stage_c(c):
         send_to(3, c, mb_s, mb_r, prv).wait_recv()
-        pat = patterns(2 * M)
+        last = lane_ids(2 * M) == LANES - 1
         u = first(field(c3, c, 0), field(c3, c, 1))
-        low, high = lat_split(3, lon_split(u, tiles_of(mb_r[c])), pat)
+        low, high = lat_split(3, lon_split(u, tiles_of(mb_r[c])), forth, last)
         low = [low[0] * wc[...]]
         high = [high[0] * wh3[...]]
-        u, t = lon_join(lat_join(3, low, high, pat))
+        u, t = lon_join(lat_join(3, low, high, back, last))
         u3[c] = wide(u)
         mc_s[c] = wide(t)
         send_to(4, c, mc_s, mc_r, nxt).start()
 
-    def synthesis(level, c, p, coarse, bands, highs, pat):
-        return lon_join(
-            lat_join(level, stack(field(coarse, c, p), field(bands, c, p)), field(highs, c, p), pat)
-        )
+    def synthesis(level, c, ps, coarse, bands, highs):
+        rows = 2 * M
+        last = lane_ids(rows * len(ps)) == LANES - 1
+        low = [stack(field(coarse, c, p), field(bands, c, p)) for p in ps]
+        high = [field(highs, c, p) for p in ps]
+        if len(ps) > 1:
+            low, high = [stack(*low)], [stack(*high)]
+        tiles = lat_join(level, low[0], high[0], back, last)
+        return [
+            lon_join([x[rows * n : rows * (n + 1)] for x in tiles]) for n in range(len(ps))
+        ]
 
     def put(ref, c, p, u, t):
         ref[c, 2 * p] = wide(first(u, t))
@@ -342,39 +344,34 @@
 
     def stage_d(c):
         send_to(4, c, mc_s, mc_r, nxt).wait_recv()
-        pat = patterns(2 * M)
         lane = lane_ids(M)
         put(c3, c, 0, tiles_of(u3[c]), tiles_of(mc_r[c]))
-        u, t_two = synthesis(2, c, 0, c3, b2, g2, pat)
+        (u, t_two), (u_two, t2) = synthesis(2, c, (0, 1), c3, b2, g2)
         u2[c] = wide(u)
-        u, t2 = synthesis(2, c, 1, c3, b2, g2, pat)
-        put(c2, c, 1, u, t_two)
-        u, t_one = synthesis(1, c, 2, c2, b1, g1, pat)
+        put(c2, c, 1, u_two, t_two)
+        (u, t_one), (u_one, t1) = synthesis(1, c, (2, 3), c2, b1, g1)
         u1[c] = wide(u)
-        u, t1 = synthesis(1, c, 3, c2, b1, g1, pat)
-        put(c1, c, 3, u, t_one)
-        u, t0 = synthesis(0, c, 7, c1, b0, g0, pat)
+        put(c1, c, 3, u_one, t_one)
+        ((u, t0),) = synthesis(0, c, (7,), c1, b0, g0)
         ul[c] = wide(u)
-        halo = jnp.where(lane < 64, t1[4], roll(t2[2], 64))
+        halo = jnp.where(lane < 64, roll(t2[2], 64), t1[4])
         md_s[c] = wide(t0 + t1[:4] + t2[:2] + [halo])
         send_to(5, c, md_s, md_r, nxt).start()
 
     def stage_e(c):
         send_to(5, c, md_s, md_r, nxt).wait_recv()
-        pat = patterns(2 * M)
         got = tiles_of(md_r[c])
         halo = got[14]
-        t0, t1, t2 = got[:8], got[8:12] + [halo], got[12:14] + [roll(halo, -64)]
+        t0, t1, t2 = got[:8], got[8:12] + [halo], got[12:14] + [roll(halo, 64)]
         put(c2, c, 0, tiles_of(u2[c]), t2)
         t = t1
-        for p in (0, 1):
-            u, t_next = synthesis(1, c, p, c2, b1, g1, pat)
+        for p, (u, t_next) in enumerate(synthesis(1, c, (0, 1), c2, b1, g1)):
             put(c1, c, p, u, t)
             t = t_next
         put(c1, c, 2, tiles_of(u1[c]), t)
         t = t0
         for p in range(7):
-            u, t_next = synthesis(0, c, p, c1, b0, g0, pat)
+            ((u, t_next),) = synthesis(0, c, (p,), c1, b0, g0)
             put(oxt, c, p, u, t)
             t = t_next
         put(oxt, c, 7, tiles_of(ul[c]), t)
@@ -391,7 +388,7 @@
             side_copy().wait_recv()
 
         pat = patterns(TABLE_ROWS)
-        lane, front, even_odd, odd_even, _, _ = pat
+        lane, front, even_odd, odd_even = pat
 
         def halved(tiles):
             if len(tiles) == 1:
@@ -401,17 +398,17 @@
                 for a, b in zip(tiles[::2], tiles[1::2])
             ]
 
-        def between(x, lo, hi):
-            return jnp.where((lane >= lo) & (lane < hi) & has_left, x, 0.0)
+        def after(x, lo):
+            return jnp.where((lane >= lo) & has_left, x, 0.0)
 
         main, edge = tiles_of(table[...]), side[...]
-        tab0[...] = wide(main + [between(roll(edge, 32), 16, 32)]) * H0**4
-        main, edge = halved(main), permute(edge, even_odd)
-        tab1[...] = wide(main + [between(roll(edge, 80), 8, 16)]) * H0**8
-        main, edge = halved(main), permute(edge, even_odd)
-        tab2[...] = wide(main + [between(roll(edge, 104), 4, 8)]) * H0**12
-        main, edge = halved(main), permute(edge, even_odd)
-        tab3[...] = jnp.where(lane < 64, main[0], between(roll(edge, 52), 66, 68)) * H0**16
+        tab0[...] = wide(main + [after(edge, 112)]) * H0**4
+        main, edge = halved(main), permute(edge, odd_even)
+        tab1[...] = wide(main + [after(edge, 120)]) * H0**8
+        main, edge = halved(main), permute(edge, odd_even)
+        tab2[...] = wide(main + [after(edge, 124)]) * H0**12
+        main, edge = halved(main), permute(edge, odd_even)
+        tab3[...] = jnp.where(lane < 64, main[0], after(edge, 126)) * H0**16
 
         def row(tab, i):
             one = tab[pl.ds(band_index[i], 1), :]
@@ -428,6 +425,7 @@
 
     lax.fori_loop(0, OFFSETS[1], lambda c, carry: (stage_z(c), carry)[1], 0)
     weights()
+    matrix_copy.wait()
 
     def step(s, carry):
         for stage, offset in zip((stage_z, stage_a, stage_b, stage_c, stage_d, stage_e), OFFSETS):
@@ -495,14 +493,16 @@
             pl.BlockSpec(memory_space=pl.ANY),
             pl.BlockSpec(memory_space=pltpu.VMEM),
             pl.BlockSpec(memory_space=pltpu.SMEM),
+            pl.BlockSpec(memory_space=pl.ANY),
         ],
         out_specs=pl.BlockSpec(memory_space=pl.ANY),
         scratch_shapes=per + weights + tables + messages
-        + [dma((chunks,)), dma((chunks,)), dma((6, chunks)), dma((6, chunks)), dma, dma],
+        + [pltpu.VMEM((2, 6 * LANES, 2 * LANES), jnp.bfloat16)]
+        + [dma((chunks,)), dma((chunks,)), dma((6, chunks)), dma((6, chunks)), dma, dma, dma],
         compiler_params=pltpu.CompilerParams(
             collective_id=0, has_side_effects=True, vmem_limit_bytes=60 * 2**20
         ),
-    )(perturbation, weight_table, band_index)
+    )(perturbation, weight_table, band_index, jnp.asarray(filter_matrices()))
 
 
 def solution(mesh):

time: 74 us -> 61.8 us (0.84)
  Pallas kernels: 68.1 us -> 55.9 us
    pallas_call x1, Pallas kernels: 68.1 us -> 55.9 us  [per_device(): pl.pallas_call(kernel, out_shape=jax.ShapeDtypeStruct(perturbation.shape,...]
where the time goes in v2:
time: 61.8 us; the launch traced here: 61.6 us
  Pallas kernels  55.9 us (90%)
  local copies, waits for them, and re-layouts  5.7 us (9%)
    pallas_call x1, Pallas kernels, per_device(): pl.pallas_call(kernel, out_shape=jax.ShapeDtypeStruct(perturbation.shape,...  55.9 us
    unnamed x1, local copies, waits for them, and re-layouts  5.7 us

profile of v2, /device:TPU:1, one launch (start us, length us, event | category | flops | bytes accessed | tf_op | source)
XLA Modules:
  0.0 61.6 jit_solution(13431308495566924533)
XLA Ops:
  0.0 55.9 %shard_map.46 = f32[80,16,1024]{2,1,0:T(8,128)} custom-call(f32[80,16,1024]{2,1,0:T(8,128)} %x_hbm.1, f32[8,512]{1,0:T(8,128)} %table.1, s32[13]{0:T(128)} %band_index.1, bf16[2,768,256]{2,1,0:T(8,128)(2,1)} %constant.2.clone.matrix_hbm), custom_call_target="tpu_custom_call" | custom-call | tf_op jit(solution)/shard_map/pallas_call | solution.py:489
  55.9 5.7 %copy.6 = f32[80,16,1024]{2,1,0:T(8,128)} copy(f32[80,16,1024]{2,1,0:T(8,128)} %shard_map.46) | data formatting | bytes 10485760

commit v3 on v2

--- a/solution.py
+++ b/solution.py
@@ -129,7 +129,7 @@
     c1, c2, c3, g0, g1, g2, b0, b1, b2,
     wh0, wh1, wh2, wh3, wb0, wb1, wb2, wb3, wc,
     tab0, tab1, tab2, tab3, side,
-    hl_s, hl_r, hr_s, hr_r, ma_s, ma_r, mb_s, mb_r, mc_s, mc_r, md_s, md_r,
+    hl_s, hl_r, hr_s, hr_r, mz_s, mz_r, me_s, me_r, ma_s, ma_r, mb_s, mb_r, mc_s, mc_r, md_s, md_r,
     matrices, in_sem, out_sem, send, recv, side_send, side_recv, matrix_sem,
 ):
     chunks = xin.shape[0]
@@ -196,6 +196,8 @@
 
     def stage_z(c):
         pltpu.make_async_copy(x_hbm.at[pl.ds(M * c, M)], xin.at[c], in_sem.at[c]).wait()
+        mz_s[c] = Q * xin[c, 0] - xin[c, 1]
+        send_to(6, c, mz_s, mz_r, prv).start()
         quarter = lane_ids(M) >> 5
         for k in range(LON // 4):
             to_left = to_right = None
@@ -269,7 +271,7 @@
             xh[c, i] = jnp.where(in_front, roll(r_part, -HALO * n), rest)
 
         x0, x1 = input_field(c, 0), input_field(c, 1)
-        t0 = second(x0, x1)
+        t0 = Q * x0[8] - x1[8]
         u = first(x0, x1)
         for p in range(7):
             x0, x1 = input_field(c, 2 * p + 2), input_field(c, 2 * p + 3)
@@ -287,20 +289,21 @@
         two(1, (0, 1), c, pair, c2, b1, g1, wb1, wh1)
         t2 = second(field(c2, c, 0), field(c2, c, 1))
         halo = jnp.where(lane < 32, roll(t2[2], 32), roll(t1[4], 64))
-        halo = jnp.where(lane < 64, halo, t0[8])
-        ma_s[c] = wide(t0[:8] + t1[:4] + t2[:2] + [halo])
+        halo = jnp.where(lane < 64, halo, t0)
+        ma_s[c] = wide(t1[:4] + t2[:2] + [halo])
         send_to(2, c, ma_s, ma_r, prv).start()
 
     def stage_b(c):
+        send_to(6, c, mz_s, mz_r, prv).wait_recv()
         send_to(2, c, ma_s, ma_r, prv).wait_recv()
         last = lane_ids(2 * M) == LANES - 1
         lane = lane_ids(M)
         got = tiles_of(ma_r[c])
-        halo = got[14]
+        halo = got[6]
         h0 = jnp.where(lane < 32, roll(halo, 64), halo)
         h1 = jnp.where(lane < 64, roll(halo, 96), roll(halo, 64))
         h2 = jnp.where(lane < 64, roll(halo, 112), roll(halo, 96))
-        t0, t1, t2 = got[:8] + [h0], got[8:12] + [h1], got[12:14] + [h2]
+        t0, t1, t2 = tiles_of(mz_r[c]) + [h0], got[:4] + [h1], got[4:6] + [h2]
         low, high = lat_split(0, lon_split(tiles_of(u0[c]), t0), forth, last)
         keep(0, 7, c, low, high, c1, b0, g0, wb0, wh0)
         x0, x1 = field(c1, c, 6), field(c1, c, 7)
@@ -352,24 +355,27 @@
         (u, t_one), (u_one, t1) = synthesis(1, c, (2, 3), c2, b1, g1)
         u1[c] = wide(u)
         put(c1, c, 3, u_one, t_one)
+        halo = jnp.where(lane < 64, roll(t2[2], 64), t1[4])
+        md_s[c] = wide(t1[:4] + t2[:2] + [halo])
+        send_to(5, c, md_s, md_r, nxt).start()
         ((u, t0),) = synthesis(0, c, (7,), c1, b0, g0)
         ul[c] = wide(u)
-        halo = jnp.where(lane < 64, roll(t2[2], 64), t1[4])
-        md_s[c] = wide(t0 + t1[:4] + t2[:2] + [halo])
-        send_to(5, c, md_s, md_r, nxt).start()
+        me_s[c] = wide(t0)
+        send_to(7, c, me_s, me_r, nxt).start()
 
     def stage_e(c):
         send_to(5, c, md_s, md_r, nxt).wait_recv()
         got = tiles_of(md_r[c])
-        halo = got[14]
-        t0, t1, t2 = got[:8], got[8:12] + [halo], got[12:14] + [roll(halo, 64)]
+        halo = got[6]
+        t1, t2 = got[:4] + [halo], got[4:6] + [roll(halo, 64)]
         put(c2, c, 0, tiles_of(u2[c]), t2)
         t = t1
         for p, (u, t_next) in enumerate(synthesis(1, c, (0, 1), c2, b1, g1)):
             put(c1, c, p, u, t)
             t = t_next
         put(c1, c, 2, tiles_of(u1[c]), t)
-        t = t0
+        send_to(7, c, me_s, me_r, nxt).wait_recv()
+        t = tiles_of(me_r[c])
         for p in range(7):
             ((u, t_next),) = synthesis(0, c, (p,), c1, b0, g0)
             put(oxt, c, p, u, t)
@@ -452,6 +458,8 @@
         send_to(3, c, mb_s, mb_r, prv).wait_send()
         send_to(4, c, mc_s, mc_r, nxt).wait_send()
         send_to(5, c, md_s, md_r, nxt).wait_send()
+        send_to(6, c, mz_s, mz_r, prv).wait_send()
+        send_to(7, c, me_s, me_r, nxt).wait_send()
         pltpu.make_async_copy(oxt.at[c], out_hbm.at[pl.ds(M * c, M)], out_sem.at[c]).wait()
         return carry
 
@@ -459,6 +467,25 @@
 
 
 TABLE_ROWS = 8
+
+
+def hand_over(y, out, held, in_sem, out_sem):
+    chunks = held.shape[0]
+    size = y.shape[0] // chunks
+
+    def load(c):
+        return pltpu.make_async_copy(y.at[pl.ds(size * c, size)], held.at[c], in_sem.at[c])
+
+    def store(c):
+        return pltpu.make_async_copy(held.at[c], out.at[pl.ds(size * c, size)], out_sem.at[c])
+
+    for c in range(chunks):
+        load(c).start()
+    for c in range(chunks):
+        load(c).wait()
+        store(c).start()
+    for c in range(chunks):
+        store(c).wait()
 
 
 def per_device(perturbation, weight_table, band_index):
@@ -482,11 +509,11 @@
     ]
     weights = [vmem(2 * M, h) for h in halves] + [vmem(M, h) for h in halves] + [vmem(2 * M, LANES)]
     tables = [vmem(TABLE_ROWS, h) for h in halves] + [vmem(TABLE_ROWS, LANES)]
-    messages = [vmem(chunks, LON // 4, M, LANES)] * 4
-    messages += [vmem(chunks, M, 15 * LANES)] * 2 + [vmem(chunks, M, 2 * LANES)] * 4
-    messages += [vmem(chunks, M, 15 * LANES)] * 2
+    messages = [vmem(chunks, LON // 4, M, LANES)] * 4 + [vmem(chunks, M, width)] * 4
+    messages += [vmem(chunks, M, 7 * LANES)] * 2 + [vmem(chunks, M, 2 * LANES)] * 4
+    messages += [vmem(chunks, M, 7 * LANES)] * 2
     dma = pltpu.SemaphoreType.DMA
-    return pl.pallas_call(
+    result = pl.pallas_call(
         kernel,
         out_shape=jax.ShapeDtypeStruct(perturbation.shape, F32),
         in_specs=[
@@ -498,11 +525,19 @@
         out_specs=pl.BlockSpec(memory_space=pl.ANY),
         scratch_shapes=per + weights + tables + messages
         + [pltpu.VMEM((2, 6 * LANES, 2 * LANES), jnp.bfloat16)]
-        + [dma((chunks,)), dma((chunks,)), dma((6, chunks)), dma((6, chunks)), dma, dma, dma],
+        + [dma((chunks,)), dma((chunks,)), dma((8, chunks)), dma((8, chunks)), dma, dma, dma],
         compiler_params=pltpu.CompilerParams(
             collective_id=0, has_side_effects=True, vmem_limit_bytes=60 * 2**20
         ),
     )(perturbation, weight_table, band_index, jnp.asarray(filter_matrices()))
+    return pl.pallas_call(
+        hand_over,
+        out_shape=jax.ShapeDtypeStruct(perturbation.shape, F32),
+        in_specs=[pl.BlockSpec(memory_space=pl.ANY)],
+        out_specs=pl.BlockSpec(memory_space=pl.ANY),
+        scratch_shapes=[vmem(10, members // 10, LON, width), dma((10,)), dma((10,))],
+        compiler_params=pltpu.CompilerParams(vmem_limit_bytes=60 * 2**20),
+    )(result)
 
 
 def solution(mesh):

time: 61.8 us -> 62 us (level)
  the two profiles are of different devices: /device:TPU:1 before, /device:TPU:4 now
where the time goes in v3:
time: 62 us; the launch traced here: 61.8 us
  Pallas kernels  61.8 us (100%)
    pallas_call x1, Pallas kernels, per_device(): pl.pallas_call(kernel, out_shape=jax.ShapeDtypeStruct(perturbation.shape,...  57.1 us
    pallas_call x1, Pallas kernels, per_device(): pl.pallas_call(hand_over, out_shape=jax.ShapeDtypeStruct(perturbation.sha...  4.71 us

profile of v3, /device:TPU:4, one launch (start us, length us, event | category | flops | bytes accessed | tf_op | source)
XLA Modules:
  0.0 61.8 jit_solution(10028433353405131025)
XLA Ops:
  0.0 57.1 %shard_map.46.y = f32[80,16,1024]{2,1,0:T(8,128)} custom-call(f32[80,16,1024]{2,1,0:T(8,128)} %x_hbm.1, f32[8,512]{1,0:T(8,128)} %table.1, s32[13]{0:T(128)} %band_index.1, bf16[2,768,256]{2,1,0:T(8,128)(2,1)} %constant.2.clone.matrix_hbm), custom_call_target="tpu_custom_call" | custom-call | tf_op jit(solution)/shard_map/pallas_call | solution.py:516
  57.1 4.7 %shard_map.47 = f32[80,16,1024]{2,1,0:T(8,128)} custom-call(f32[80,16,1024]{2,1,0:T(8,128)} %shard_map.46.y), custom_call_target="tpu_custom_call" | custom-call | tf_op jit(solution)/shard_map/pallas_call | solution.py:533
